TPU v7x, 8 devices: a whole 2x2x1 slice. The times are simulated.
8 devices in a mesh: data: 2 (over z, y), tp: 4 (over x, core).
Axes of the slice: x: 2, y: 2, z: 1, core: 2. Of those that a mesh axis runs over, the one named last changes fastest.
Arguments:
- x_tokens: bfloat16 [512, 5120], P(('data', 'tp')), parts along dimension 0
- ln_gamma: float32 [5120], replicated
- w_qkv: bfloat16 [5120, 40, 384], P(None, 'tp')
- w_out: bfloat16 [40, 128, 5120], P('tp')
- w_up: bfloat16 [5120, 13824], P(None, 'tp')
- w_down: bfloat16 [13824, 5120], P('tp')
Outputs:
- output: bfloat16 [512, 5120], P(('data', 'tp')), parts along dimension 0
There are 2 independent parts. A program takes and returns all parts, laid end to end along the dimension named above; an argument that names none is the same for every part.
All inputs are finite; a program needn't handle non-finite values.
Results may differ from a plain program's by a relative error of at most 0.0027405.
Values are sent between devices in bfloat16 or wider.
A program may use at most 1 GiB of HBM per device.

v0:
```python
import math
import jax
import jax.numpy as jnp
from jax import lax
from jax.sharding import PartitionSpec as P

LN_EPS = 1e-6


def layer_norm(row_vals, ln_gain):
    row_mean = jnp.mean(row_vals, axis=-1, keepdims=True)
    centered = row_vals - row_mean
    row_var = jnp.mean(centered * centered, axis=-1, keepdims=True)
    return (centered * lax.rsqrt(row_var + LN_EPS) * ln_gain).astype(jnp.bfloat16)


def block_rows(row_count, head_count):
    return min(row_count, 2 ** int(math.log2(max(8, 4096 // head_count))))


def attend(query_rows, key_rows, value_rows):
    row_count, head_count, head_dim = query_rows.shape
    q_size = block_rows(row_count, head_count)
    attn_scale = head_dim ** -0.5

    def one_block(query_blk):
        scores = jnp.einsum("qhe,khe->hqk", query_blk, key_rows, preferred_element_type=jnp.float32) * attn_scale
        row_max = jnp.max(scores, axis=-1, keepdims=True)
        exp_scores = jnp.exp(scores - row_max)
        exp_sum = jnp.sum(exp_scores, axis=-1, keepdims=True)
        block_out = jnp.einsum("hqk,khe->hqe", exp_scores.astype(jnp.bfloat16), value_rows, preferred_element_type=jnp.float32)
        return (block_out / exp_sum).astype(jnp.bfloat16)

    return lax.map(one_block, query_rows.reshape(row_count // q_size, q_size, head_count, head_dim))


def solution(mesh):
    def local_block(x_loc, ln_gamma, w_qkv, w_out, w_up, w_down):
        model_dim = x_loc.shape[1]
        head_dim = w_qkv.shape[2] // 3
        residual = x_loc.astype(jnp.float32)
        normed = layer_norm(residual, ln_gamma)
        gathered = lax.all_gather(normed, "tp", axis=0, tiled=True)
        seq_len = gathered.shape[0]
        qkv_rows = jnp.einsum("sd,dhc->shc", gathered, w_qkv, preferred_element_type=jnp.float32).astype(jnp.bfloat16)
        head_out = attend(qkv_rows[:, :, :head_dim], qkv_rows[:, :, head_dim:2 * head_dim], qkv_rows[:, :, 2 * head_dim:])
        attn_part = jnp.einsum("nhqe,hed->nqd", head_out, w_out, preferred_element_type=jnp.float32).reshape(seq_len, model_dim)
        pre_act = jnp.dot(gathered, w_up, preferred_element_type=jnp.float32)
        hidden = jax.nn.gelu(pre_act, approximate=True).astype(jnp.bfloat16)
        part_sum = attn_part + jnp.dot(hidden, w_down, preferred_element_type=jnp.float32)
        reduced = lax.psum_scatter(part_sum, "tp", scatter_dimension=0, tiled=True)
        return (residual + reduced).astype(jnp.bfloat16)

    row_spec = P(("data", "tp"), None)
    return jax.shard_map(local_block, mesh=mesh, in_specs=(row_spec, P(None), P(None, "tp", None), P("tp", None, None), P(None, "tp"), P("tp", None)), out_specs=row_spec, check_vma=False)
```

profile of v0, /device:TPU:0, one launch (start us, length us, event | category | flops | bytes accessed | tf_op | source)
XLA Modules:
  0.0 159.2 jit_solution(371905563078125180)
XLA Ops:
  6.5 0.0 all-gather.2.cloned.1.call-start
  6.5 1.3 convert_reduce_fusion
  7.8 1.4 fusion.25
  9.3 2.2 %fusion.27 = bf16[64,5120]{1,0:T(8,128)(2,1)} fusion(bf16[64,5120]{1,0:T(8,128)(2,1)} %param.6, f32[5120]{0:T(1024)} %param.7, f32[64]{0:T(128)S(1)} %add_rsqrt_fusion, f32[64]{0:T(128)S(1)} %broadcast_multiply_fusion), kind=kLoop, calls=%fused_computation.32 | loop fusion | flops 1638400 | bytes 1331712 | tf_op jit(solution)/shard_map/convert_element_type | solution.py:14
  11.5 0.0 all-gather.2.cloned.1.call-update
  11.5 0.0 reduce-scatter.2.cloned.1.call-start
  11.5 25.4 %all-gather.2.cloned.1.call-done = bf16[256,5120]{1,0:T(8,128)(2,1)} async-done(((bf16[64,5120]{1,0:T(8,128)(2,1)}), bf16[256,5120]{1,0:T(8,128)(2,1)}) %all-gather.2.cloned.1.call-update) | async-done | bytes 2621456 | tf_op jit(solution)/shard_map/all_gather | solution.py:43
  36.9 19.6 %fusion.13 = bf16[256,10,384]{2,0,1:T(8,128)(2,1)} fusion(bf16[5120,10,384]{2,0,1:T(8,128)(2,1)} %param.8, bf16[256,5120]{1,0:T(8,128)(2,1)} %all-gather.2.cloned.1.call-done), kind=kOutput, calls=%fused_computation.20 | convolution fusion | flops 10067312640 | bytes 43909120 | tf_op jit(solution)/shard_map/sd,dhc->shc/dot_general | solution.py:45
  56.5 1.8 %multiply_reduce_fusion = (f32[10,256]{1,0:T(8,128)S(1)}, f32[10,256,256]{1,2,0:T(8,128)S(1)}) fusion(bf16[256,10,384]{2,0,1:T(8,128)(2,1)} %fusion.13), kind=kOutput, calls=%fused_computation.14 | convolution fusion | flops 169080320 | bytes 3942400 | tf_op jit(solution)/shard_map/while/body/eval_jaxpr/qhe,khe->hqk/dot_general | solution.py:27
  58.2 0.4 fusion.11
  58.7 36.1 %fusion.16 = f32[256,5120]{1,0:T(8,128)} fusion(bf16[3456,5120]{1,0:T(8,128)(2,1)} %param.11, bf16[256,5120]{1,0:T(8,128)(2,1)} %all-gather.2.cloned.1.call-done, bf16[5120,3456]{1,0:T(8,128)(2,1)} %param.10), kind=kOutput, calls=%fused_computation.21 | convolution fusion | flops 18127355904 | bytes 78643200 | tf_op jit(solution)/shard_map/dot_general | solution.py:50
  94.8 10.4 %fusion = f32[256,5120]{1,0:T(8,128)} fusion(f32[256,5120]{1,0:T(8,128)} %fusion.16, bf16[10,128,5120]{2,1,0:T(8,128)(2,1)} %param.9, f32[10,256,256]{1,2,0:T(8,128)S(1)} %get-tuple-element.14, f32[10,256]{1,0:T(8,128)S(1)} %get-tuple-element.13, bf16[256,10,384]{2,0,1:T(8,128)(2,1)} %fusion.13, f32[10,256]{1,0:T(8,128)S(1)} %fusion.11), kind=kOutput, calls=%fused_computation.1 | convolution fusion | flops 3527147520 | bytes 26890240 | tf_op jit(solution)/shard_map/nhqe,hed->nqd/dot_general | solution.py:47
  105.1 0.0 copy-start
  105.1 0.0 reduce-scatter.2.cloned.1.call-update
  105.1 45.0 %reduce-scatter.2.cloned.1.call-done = f32[64,5120]{1,0:T(8,128)} async-done(((f32[256,5120]{1,0:T(8,128)}), f32[64,5120]{1,0:T(8,128)}) %reduce-scatter.2.cloned.1.call-update) | async-done | bytes 1310736 | tf_op jit(solution)/shard_map/reduce_scatter | solution.py:51
  150.1 0.0 copy-done
  150.1 2.3 %fusion.28 = bf16[64,5120]{1,0:T(8,128)(2,1)} fusion(f32[64,5120]{1,0:T(8,128)} %reduce-scatter.2.cloned.1.call-done, bf16[64,5120]{1,0:T(8,128)(2,1)S(1)} %copy-done), kind=kLoop, calls=%fused_computation.33 | loop fusion | flops 983040 | bytes 2621440 | tf_op jit(solution)/shard_map/convert_element_type | solution.py:52
  (2 shorter events, 0.0 us)
Async XLA Ops:
  6.5 30.4 %all-gather.2.cloned.1.call-start = ((), (), s32[]{:S(2)}) async-start(), calls=%async_computation.1 | async-start | bytes 3276800 | tf_op jit(solution)/shard_map/all_gather | solution.py:43
  11.5 138.6 %reduce-scatter.2.cloned.1.call-start = ((), (), s32[]{:S(2)}) async-start(), calls=%async_computation.2 | async-start | bytes 6553600 | tf_op jit(solution)/shard_map/reduce_scatter | solution.py:51
  105.1 45.0 %copy-start = (bf16[64,5120]{1,0:T(8,128)(2,1)S(1)}, bf16[64,5120]{1,0:T(8,128)(2,1)}, u32[]{:S(2)}) copy-start(bf16[64,5120]{1,0:T(8,128)(2,1)} %param.6) | copy-start | bytes 1966084
Sparse Core Ops, SparseCore 0:
  11.6 25.2 all-gather.1
  105.3 44.8 reduce-scatter.1
where the time goes:
time: 159 us
  waiting for transfers between devices  70.4 us (44%)
  matrix products  67.8 us (43%)
  between operations  13.4 us (8%)
  other arithmetic  7.61 us (5%)
    reduce_scatter x1, waiting for transfers between devices, local_block(): reduced = lax.psum_scatter(part_sum, 'tp', scatter_dimension=0, tiled=True)  45 us
    dot_general x1, matrix products, local_block(): jnp.dot(hidden, w_down, preferred_element_type=jnp.float32)  36.1 us
    all_gather x1, waiting for transfers between devices, local_block(): gathered = lax.all_gather(normed, 'tp', axis=0, tiled=True)  25.4 us
    dot_general x1, matrix products, local_block(): jnp.einsum('sd,dhc->shc', gathered, w_qkv, preferred_element_type=jnp.flo...  19.6 us
    dot_general x1, matrix products, local_block(): jnp.einsum('nhqe,hed->nqd', head_out, w_out, preferred_element_type=jnp.f...  10.4 us
  transfers between devices with their start and end apart: 2, of which 2 were waited for; matrix products, arithmetic and copies ran while one was open for 0% of the time, Pallas kernels for 0%

commit v1 on v0

v1 whole, which is shorter than its diff:
```python
import jax
import jax.numpy as jnp
from jax import lax
from jax.experimental import pallas as pl
from jax.experimental.pallas import tpu as pltpu
from jax.sharding import PartitionSpec as P

LN_EPS = 1e-6
MESH = pl.DeviceIdType.MESH
F32 = jnp.float32
BF16 = jnp.bfloat16

KC = 512
NC = 512
U_SLOTS = 3
D_SLOTS = 3


def kernel(x_ref, g_ref, wqkv_ref, wup_ref, wout_ref, wdown_ref, y_ref,
           xn, acc_qkv, acc_up, wq_buf, wu_buf, wd_buf, act,
           snd_sib, rcv_sib, snd_x, rcv_x, mine,
           sem_wq, sem_wu, sem_wo, sem_wd,
           s_sib, r_sib, s_par, r_par, s_fwd, r_fwd,
           s_rs, r_rs, s_rx, r_rx):
    rows, dim = x_ref.shape
    heads, head_dim = wqkv_ref.shape[0], wqkv_ref.shape[2] // 3
    ff = wup_ref.shape[1]
    att = heads * head_dim
    nk, nj = dim // KC, dim // NC
    d = lax.axis_index("data")
    t = lax.axis_index("tp")
    sib = (d, t + 1 - 2 * (t % 2))
    par = (d, (t + 2) % 4)
    scale = head_dim ** -0.5

    bar = pltpu.get_barrier_semaphore()
    for peer in (sib, par):
        pl.semaphore_signal(bar, inc=1, device_id=peer, device_id_type=MESH)

    def up_copies(k, slot):
        rows_k = pl.ds(k * KC, KC)
        return (
            pltpu.make_async_copy(wqkv_ref.at[:, rows_k, :], wq_buf.at[slot], sem_wq.at[slot]),
            pltpu.make_async_copy(wup_ref.at[rows_k, :], wu_buf.at[slot], sem_wu.at[slot]),
        )

    def down_copies(j, slot):
        cols = pl.ds(j * NC, NC)
        return (
            pltpu.make_async_copy(wout_ref.at[:, cols], wd_buf.at[slot, pl.ds(0, att), :], sem_wo.at[slot]),
            pltpu.make_async_copy(wdown_ref.at[:, cols], wd_buf.at[slot, pl.ds(att, ff), :], sem_wd.at[slot]),
        )

    def remote(src, dst, ssem, rsem, peer):
        return pltpu.make_async_remote_copy(
            src_ref=src, dst_ref=dst, send_sem=ssem, recv_sem=rsem,
            device_id=peer, device_id_type=MESH)

    def blk(r):
        return pl.ds(r * rows, rows)

    def to_sib(k):
        return remote(xn.at[k, blk(0), :], xn.at[k, blk(1), :], s_sib.at[k], r_sib.at[k], sib)

    def to_par(k):
        return remote(xn.at[k, blk(0), :], xn.at[k, blk(2), :], s_par.at[k], r_par.at[k], par)

    def fwd(k):
        return remote(xn.at[k, blk(2), :], xn.at[k, blk(3), :], s_fwd.at[k], r_fwd.at[k], sib)

    def rs_sib(j):
        return remote(snd_sib.at[j], rcv_sib.at[j], s_rs.at[j], r_rs.at[j], sib)

    def rs_x(j):
        return remote(snd_x.at[j], rcv_x.at[j], s_rx.at[j], r_rx.at[j], par)

    for k in range(U_SLOTS):
        for c in up_copies(k, k):
            c.start()

    @pl.loop(0, rows // 16)
    def _(i):
        r = pl.ds(pl.multiple_of(i * 16, 16), 16)
        v = x_ref[r, :].astype(F32)
        cen = v - jnp.mean(v, axis=-1, keepdims=True)
        var = jnp.mean(cen * cen, axis=-1, keepdims=True)
        n = (cen * lax.rsqrt(var + LN_EPS) * g_ref[...]).astype(BF16)
        for k in range(nk):
            xn[k, r, :] = n[:, k * KC:(k + 1) * KC]

    pl.semaphore_wait(bar, 2)

    @pl.loop(0, nk)
    def _(k):
        to_par(k).start()
        to_sib(k).start()

    acc_qkv[...] = jnp.zeros_like(acc_qkv)
    acc_up[...] = jnp.zeros_like(acc_up)

    to_par(0).wait_recv()
    fwd(0).start()

    @pl.loop(0, nk)
    def _(k):
        slot = k % U_SLOTS

        @pl.when(k + 1 < nk)
        def _():
            to_par(k + 1).wait_recv()
            fwd(k + 1).start()

        to_sib(k).wait_recv()
        fwd(k).wait_recv()
        cq, cu = up_copies(k, slot)
        cq.wait()
        xk = xn[k]
        pair = 2 * 3 * head_dim
        for h in range(0, heads, 2):
            w = jnp.concatenate([wq_buf[slot, h], wq_buf[slot, h + 1]], axis=1)
            sl = slice(h // 2 * pair, (h // 2 + 1) * pair)
            acc_qkv[:, sl] += jnp.dot(xk, w, preferred_element_type=F32)
        cu.wait()
        for n in range(0, ff, pair):
            sl = slice(n, min(n + pair, ff))
            acc_up[:, sl] += jnp.dot(xk, wu_buf[slot, :, sl], preferred_element_type=F32)

        @pl.when(k + U_SLOTS < nk)
        def _():
            for c in up_copies(k + U_SLOTS, slot):
                c.start()

        @pl.when(k + U_SLOTS >= nk)
        def _():
            j = k + U_SLOTS - nk
            for c in down_copies(j, j):
                c.start()

    for h in range(heads):
        o = h * 3 * head_dim
        q = acc_qkv[:, o:o + head_dim].astype(BF16)
        kk = acc_qkv[:, o + head_dim:o + 2 * head_dim].astype(BF16)
        vv = acc_qkv[:, o + 2 * head_dim:o + 3 * head_dim].astype(BF16)
        s = lax.dot_general(q, kk, (((1,), (1,)), ((), ())), preferred_element_type=F32) * scale
        e = jnp.exp(s - jnp.max(s, axis=-1, keepdims=True))
        l = jnp.sum(e, axis=-1, keepdims=True)
        ov = jnp.dot(e.astype(BF16), vv, preferred_element_type=F32)
        act[:, h * head_dim:(h + 1) * head_dim] = (ov / l).astype(BF16)

    n_rows = act.shape[0]

    @pl.loop(0, n_rows // 16)
    def _(i):
        r = pl.ds(pl.multiple_of(i * 16, 16), 16)
        act[r, att:] = jax.nn.gelu(acc_up[r, :], approximate=True).astype(BF16)

    def combine(j):
        rs_sib(j).wait_recv()
        snd_x[j] = snd_x[j] + rcv_sib[j, 0]
        mine[j] = mine[j] + rcv_sib[j, 1]

    @pl.loop(0, nj)
    def _(j):
        slot = j % D_SLOTS
        co, cd = down_copies(j, slot)
        co.wait()
        cd.wait()
        p = jnp.dot(act[...], wd_buf[slot], preferred_element_type=F32)
        mine[j] = p[0:rows]
        snd_sib[j, 1] = p[rows:2 * rows]
        snd_x[j] = p[2 * rows:3 * rows]
        snd_sib[j, 0] = p[3 * rows:4 * rows]

        @pl.when(j > 0)
        def _():
            combine(j - 1)

        rs_sib(j).start()

        @pl.when(j > 0)
        def _():
            rs_x(j - 1).start()

        @pl.when(j + D_SLOTS < nj)
        def _():
            for c in down_copies(j + D_SLOTS, slot):
                c.start()

    combine(nj - 1)
    rs_x(nj - 1).start()

    for j in range(nj):
        rs_x(j).wait_recv()
        cols = slice(j * NC, (j + 1) * NC)
        y_ref[:, cols] = (x_ref[:, cols].astype(F32) + (mine[j] + rcv_x[j])).astype(BF16)

    @pl.loop(0, nk)
    def _(k):
        to_sib(k).wait_send()
        to_par(k).wait_send()
        fwd(k).wait_send()

    @pl.loop(0, nj)
    def _(j):
        rs_sib(j).wait_send()
        rs_x(j).wait_send()


def solution(mesh):
    def local_block(x_loc, ln_gamma, w_qkv, w_out, w_up, w_down):
        rows, dim = x_loc.shape
        heads, hd3 = w_qkv.shape[1:]
        att = heads * hd3 // 3
        ff = w_up.shape[1]
        seq = 4 * rows
        nk, nj = dim // KC, dim // NC
        vm = pl.BlockSpec(memory_space=pltpu.VMEM)
        hbm = pl.BlockSpec(memory_space=pl.ANY)
        dma = pltpu.SemaphoreType.DMA
        return pl.pallas_call(
            kernel,
            out_shape=jax.ShapeDtypeStruct((rows, dim), BF16),
            in_specs=[vm, vm, hbm, hbm, hbm, hbm],
            out_specs=vm,
            scratch_shapes=[
                pltpu.VMEM((nk, seq, KC), BF16),
                pltpu.VMEM((seq, heads * hd3), F32),
                pltpu.VMEM((seq, ff), F32),
                pltpu.VMEM((U_SLOTS, heads, KC, hd3), BF16),
                pltpu.VMEM((U_SLOTS, KC, ff), BF16),
                pltpu.VMEM((D_SLOTS, att + ff, NC), BF16),
                pltpu.VMEM((seq, att + ff), BF16),
                pltpu.VMEM((nj, 2, rows, NC), F32),
                pltpu.VMEM((nj, 2, rows, NC), F32),
                pltpu.VMEM((nj, rows, NC), F32),
                pltpu.VMEM((nj, rows, NC), F32),
                pltpu.VMEM((nj, rows, NC), F32),
                dma((U_SLOTS,)), dma((U_SLOTS,)), dma((D_SLOTS,)), dma((D_SLOTS,)),
                dma((nk,)), dma((nk,)), dma((nk,)), dma((nk,)), dma((nk,)), dma((nk,)),
                dma((nj,)), dma((nj,)), dma((nj,)), dma((nj,)),
            ],
            compiler_params=pltpu.CompilerParams(
                collective_id=0, has_side_effects=True, vmem_limit_bytes=66_900_000),
            cost_estimate=pl.CostEstimate(flops=32 * 10**9, bytes_accessed=125 * 10**6, transcendentals=10**6),
            name="block",
        )(x_loc, ln_gamma.reshape(1, dim), jnp.transpose(w_qkv, (1, 0, 2)), w_up,
          w_out.reshape(att, dim), w_down)

    row_spec = P(("data", "tp"), None)
    return jax.shard_map(
        local_block, mesh=mesh,
        in_specs=(row_spec, P(None), P(None, "tp", None), P("tp", None, None), P(None, "tp"), P("tp", None)),
        out_specs=row_spec, check_vma=False)
```

time: 159 us -> 74.2 us (0.47)
  Pallas kernels: 0 us -> 72.1 us
  waiting for transfers between devices: 70.4 us -> 0 us
  matrix products: 67.8 us -> 0 us
  between operations: 13.4 us -> 0.01 us
  other arithmetic: 7.61 us -> 0 us
  local copies, waits for them, and re-layouts: 0.01 us -> 1.97 us
    pallas_call x0 -> x1, Pallas kernels: none -> 72.1 us  [local_block(): pl.pallas_call(kernel, out_shape=jax.ShapeDtypeStruct((rows, dim), BF16),...]
    dot_general x4 -> x0, matrix products: 67.8 us -> none  [the longest x1 36.1 us: local_block(): jnp.dot(hidden, w_down, preferred_element_type=jnp.float32)]
    reduce_scatter x1 -> x0, waiting for transfers between devices: 45 us -> none  [local_block(): reduced = lax.psum_scatter(part_sum, 'tp', scatter_dimension=0, tiled=True)]
    all_gather x1 -> x0, waiting for transfers between devices: 25.4 us -> none  [local_block(): gathered = lax.all_gather(normed, 'tp', axis=0, tiled=True)]
    convert_element_type x2 -> x0, other arithmetic: 4.45 us -> none  [the longest x1 2.26 us: local_block(): return (residual + reduced).astype(jnp.bfloat16)]
    reduce_sum x3 -> x0, other arithmetic: 3.15 us -> none  [the longest x1 1.43 us: layer_norm(): row_var = jnp.mean(centered * centered, axis=-1, keepdims=True)]
    unnamed x2 -> x1, local copies, waits for them, and re-layouts: 0.01 us -> 1.97 us
  transfers between devices with their start and end apart: 2 -> 0, of which waited for: 2 -> 0; matrix products, arithmetic and copies ran while one was open for 0% -> 0% of each run, Pallas kernels for 0% -> 0%
where the time goes in v1:
time: 74.2 us; the launch traced here: 74 us
  Pallas kernels  72.1 us (97%)
  local copies, waits for them, and re-layouts  1.97 us (3%)
    pallas_call x1, Pallas kernels, local_block(): pl.pallas_call(kernel, out_shape=jax.ShapeDtypeStruct((rows, dim), BF16),...  72.1 us
    unnamed x1, local copies, waits for them, and re-layouts  1.97 us

profile of v1, /device:TPU:0, one launch (start us, length us, event | category | flops | bytes accessed | tf_op | source)
XLA Modules:
  0.0 74.0 jit_solution(6126801143745426528)
XLA Ops:
  0.0 72.1 %block.1 = bf16[64,5120]{1,0:T(8,128)(2,1)} custom-call(bf16[64,5120]{1,0:T(8,128)(2,1)} %x_ref.1, f32[1,5120]{1,0:T(1,128)} %bitcast.5, bf16[10,5120,384]{2,1,0:T(8,128)(2,1)} %bitcast.3, bf16[5120,3456]{1,0:T(8,128)(2,1)} %wup_ref.1, bf16[1280,5120]{1,0:T(8,128)(2,1)} %bitcast.4, bf16[3456,5120]{1,0:T(8,128)(2,1)} %wdown_ref.1), custom_call_target="tpu_custom_call" | custom-call | flops 32000000000 | bytes 125000000 | tf_op jit(solution)/shard_map/block/pallas_call | solution.py:220
  72.1 2.0 %copy.8 = bf16[64,5120]{1,0:T(8,128)(2,1)} copy(bf16[64,5120]{1,0:T(8,128)(2,1)} %block.1) | data formatting | bytes 1310720

commit v2 on v1

v2 whole, which is shorter than its diff:
```python
import jax
import jax.numpy as jnp
from jax import lax
from jax.experimental import pallas as pl
from jax.experimental.pallas import tpu as pltpu
from jax.sharding import PartitionSpec as P

LN_EPS = 1e-6
MESH = pl.DeviceIdType.MESH
F32 = jnp.float32
BF16 = jnp.bfloat16

KC = 512
NC = 512
U_SLOTS = 4
LOCAL_FIRST = 3
D_SLOTS = 2


def kernel(x_hbm, g_ref, wqkv_ref, wup_ref, wout_ref, wdown_ref, y_ref,
           x_ref, stat, xn, acc_qkv, acc_up, wq_buf, wu_buf, wd_buf, act,
           snd_sc, rcv_sc, snd_so, rcv_so, snd_x, rcv_x, mine,
           sem_in, sem_wq, sem_wu, sem_wo, sem_wd,
           s_sib, r_sib, s_par, r_par, s_fwd, r_fwd,
           s_rc, r_rc, s_ro, r_ro, s_rx, r_rx):
    rows, dim = x_ref.shape
    heads, head_dim = wqkv_ref.shape[0], wqkv_ref.shape[2] // 3
    ff = wup_ref.shape[1]
    att = heads * head_dim
    nk, nj = dim // KC, dim // NC
    d = lax.axis_index("data")
    t = lax.axis_index("tp")
    sib = (d, t + 1 - 2 * (t % 2))
    par = (d, (t + 2) % 4)
    scale = head_dim ** -0.5
    near, far = slice(0, 2 * rows), slice(2 * rows, 4 * rows)

    x_in = pltpu.make_async_copy(x_hbm, x_ref, sem_in)
    x_in.start()

    bar = pltpu.get_barrier_semaphore()
    for peer in (sib, par):
        pl.semaphore_signal(bar, inc=1, device_id=peer, device_id_type=MESH)

    def q_copy(k, slot):
        return pltpu.make_async_copy(wqkv_ref.at[:, pl.ds(k * KC, KC), :], wq_buf.at[slot], sem_wq.at[slot])

    def u_copy(k, slot):
        return pltpu.make_async_copy(wup_ref.at[pl.ds(k * KC, KC), :], wu_buf.at[slot], sem_wu.at[slot])

    def down_copies(j, slot):
        cols = pl.ds(j * NC, NC)
        return (
            pltpu.make_async_copy(wout_ref.at[:, cols], wd_buf.at[slot, pl.ds(0, att), :], sem_wo.at[slot]),
            pltpu.make_async_copy(wdown_ref.at[:, cols], wd_buf.at[slot, pl.ds(att, ff), :], sem_wd.at[slot]),
        )

    def remote(src, dst, ssem, rsem, peer):
        return pltpu.make_async_remote_copy(
            src_ref=src, dst_ref=dst, send_sem=ssem, recv_sem=rsem,
            device_id=peer, device_id_type=MESH)

    def blk(r):
        return pl.ds(r * rows, rows)

    def to_sib(k):
        return remote(xn.at[k, blk(0), :], xn.at[k, blk(1), :], s_sib.at[k], r_sib.at[k], sib)

    def to_par(k):
        return remote(xn.at[k, blk(0), :], xn.at[k, blk(2), :], s_par.at[k], r_par.at[k], par)

    def fwd(k):
        return remote(xn.at[k, blk(2), :], xn.at[k, blk(3), :], s_fwd.at[k], r_fwd.at[k], sib)

    def rs_cross(j):
        return remote(snd_sc.at[j], rcv_sc.at[j], s_rc.at[j], r_rc.at[j], sib)

    def rs_own(j):
        return remote(snd_so.at[j], rcv_so.at[j], s_ro.at[j], r_ro.at[j], sib)

    def rs_x(j):
        return remote(snd_x.at[j], rcv_x.at[j], s_rx.at[j], r_rx.at[j], par)

    for k in range(U_SLOTS):
        q_copy(k, k).start()
        u_copy(k, k).start()

    x_in.wait()
    for i in range(rows // 16):
        r = slice(i * 16, (i + 1) * 16)
        v = x_ref[r, :].astype(F32)
        mean = jnp.mean(v, axis=-1, keepdims=True)
        cen = v - mean
        var = jnp.mean(cen * cen, axis=-1, keepdims=True)
        stat[0, r, :] = mean
        stat[1, r, :] = lax.rsqrt(var + LN_EPS)

    def normalize(k):
        c = slice(k * KC, (k + 1) * KC)
        cen = x_ref[:, c].astype(F32) - stat[0]
        xn[k, 0:rows, :] = (cen * stat[1] * g_ref[:, c]).astype(BF16)

    def send(k):
        to_par(k).start()
        to_sib(k).start()

    normalize(0)
    pl.semaphore_wait(bar, 2)
    for k in range(1, nk):
        normalize(k)
        send(k - 1)
    acc_qkv[near] = jnp.zeros_like(acc_qkv[near])
    send(nk - 1)
    acc_qkv[far] = jnp.zeros_like(acc_qkv[far])
    acc_up[...] = jnp.zeros_like(acc_up)

    pair = 2 * 3 * head_dim

    def up_q(k, slot, r):
        xk = xn[k, r, :]
        for h in range(0, heads, 2):
            w = jnp.concatenate([wq_buf[slot, h], wq_buf[slot, h + 1]], axis=1)
            sl = slice(h // 2 * pair, (h // 2 + 1) * pair)
            acc_qkv[r, sl] += jnp.dot(xk, w, preferred_element_type=F32)

    def up_u(k, slot, r):
        xk = xn[k, r, :]
        for n in range(0, ff, pair):
            sl = slice(n, min(n + pair, ff))
            acc_up[r, sl] += jnp.dot(xk, wu_buf[slot, :, sl], preferred_element_type=F32)

    @pl.loop(0, LOCAL_FIRST)
    def _(k):
        to_sib(k).wait_recv()
        q_copy(k, k).wait()
        up_q(k, k, near)
        u_copy(k, k).wait()
        up_u(k, k, near)

        @pl.when(k > 0)
        def _():
            to_par(k - 1).wait_recv()
            fwd(k - 1).start()

    def refill(k, slot, copy):
        @pl.when(k + U_SLOTS < nk)
        def _():
            copy(k + U_SLOTS, slot).start()

    @pl.loop(0, LOCAL_FIRST)
    def _(k):
        to_par(k + LOCAL_FIRST - 1).wait_recv()
        fwd(k + LOCAL_FIRST - 1).start()
        fwd(k).wait_recv()
        up_q(k, k, far)
        refill(k, k, q_copy)
        up_u(k, k, far)
        refill(k, k, u_copy)

    @pl.loop(LOCAL_FIRST, nk)
    def _(k):
        slot = k % U_SLOTS
        nf = k + LOCAL_FIRST - 1

        @pl.when(nf < nk)
        def _():
            to_par(nf).wait_recv()
            fwd(nf).start()

        to_sib(k).wait_recv()
        fwd(k).wait_recv()
        q_copy(k, slot).wait()
        up_q(k, slot, slice(None))
        refill(k, slot, q_copy)
        u_copy(k, slot).wait()
        up_u(k, slot, slice(None))
        refill(k, slot, u_copy)

        @pl.when(k + D_SLOTS >= nk)
        def _():
            j = k + D_SLOTS - nk
            for c in down_copies(j, j):
                c.start()

    def attention(qr):
        for h in range(heads):
            o = h * 3 * head_dim
            q = acc_qkv[qr, o:o + head_dim].astype(BF16)
            kk = acc_qkv[:, o + head_dim:o + 2 * head_dim].astype(BF16)
            vv = acc_qkv[:, o + 2 * head_dim:o + 3 * head_dim].astype(BF16)
            s = lax.dot_general(q, kk, (((1,), (1,)), ((), ())), preferred_element_type=F32) * scale
            e = jnp.exp(s - jnp.max(s, axis=-1, keepdims=True))
            l = jnp.sum(e, axis=-1, keepdims=True)
            ov = jnp.dot(e.astype(BF16), vv, preferred_element_type=F32)
            act[qr, h * head_dim:(h + 1) * head_dim] = (ov / l).astype(BF16)

    def gelu(base):
        @pl.loop(0, 2 * rows // 16)
        def _(i):
            r = pl.ds(pl.multiple_of(base + i * 16, 16), 16)
            act[r, att:] = jax.nn.gelu(acc_up[r, :], approximate=True).astype(BF16)

    def put_cross(j, p):
        snd_x[j] = p[0:rows]
        snd_sc[j] = p[rows:2 * rows]

    def put_own(j, p):
        mine[j] = p[0:rows]
        snd_so[j] = p[rows:2 * rows]

    def combine(j):
        rs_cross(j).wait_recv()
        snd_x[j] = snd_x[j] + rcv_sc[j]

    attention(far)
    gelu(2 * rows)
    for j in range(D_SLOTS):
        for c in down_copies(j, j):
            c.wait()
        put_cross(j, jnp.dot(act[far], wd_buf[j], preferred_element_type=F32))
        rs_cross(j).start()
    combine(0)
    gelu(0)
    rs_x(0).start()
    attention(near)
    for j in range(D_SLOTS):
        put_own(j, jnp.dot(act[near], wd_buf[j], preferred_element_type=F32))
        if j == 0:
            combine(1)
        rs_own(j).start()
        if j == 0:
            rs_x(1).start()
        for c in down_copies(j + D_SLOTS, j):
            c.start()

    @pl.loop(D_SLOTS, nj)
    def _(j):
        slot = j % D_SLOTS
        for c in down_copies(j, slot):
            c.wait()
        p = jnp.dot(act[...], wd_buf[slot], preferred_element_type=F32)
        put_cross(j, p[far])
        put_own(j, p[near])

        @pl.when(j > D_SLOTS)
        def _():
            combine(j - 1)

        rs_cross(j).start()
        rs_own(j).start()

        @pl.when(j > D_SLOTS)
        def _():
            rs_x(j - 1).start()

        @pl.when(j + D_SLOTS < nj)
        def _():
            for c in down_copies(j + D_SLOTS, slot):
                c.start()

    combine(nj - 1)
    rs_x(nj - 1).start()

    for j in range(nj):
        cols = slice(j * NC, (j + 1) * NC)
        rs_own(j).wait_recv()
        part = x_ref[:, cols].astype(F32) + (mine[j] + rcv_so[j])
        rs_x(j).wait_recv()
        y_ref[:, cols] = (part + rcv_x[j]).astype(BF16)

    @pl.loop(0, nk)
    def _(k):
        to_sib(k).wait_send()
        to_par(k).wait_send()
        fwd(k).wait_send()

    @pl.loop(0, nj)
    def _(j):
        rs_cross(j).wait_send()
        rs_own(j).wait_send()
        rs_x(j).wait_send()


def solution(mesh):
    def local_block(x_loc, ln_gamma, w_qkv, w_out, w_up, w_down):
        rows, dim = x_loc.shape
        heads, hd3 = w_qkv.shape[1:]
        att = heads * hd3 // 3
        ff = w_up.shape[1]
        seq = 4 * rows
        nk, nj = dim // KC, dim // NC
        vm = pl.BlockSpec(memory_space=pltpu.VMEM)
        hbm = pl.BlockSpec(memory_space=pl.ANY)
        dma = pltpu.SemaphoreType.DMA
        return pl.pallas_call(
            kernel,
            out_shape=pltpu.VMEM((rows, dim), BF16),
            in_specs=[hbm, vm, hbm, hbm, hbm, hbm],
            out_specs=vm,
            scratch_shapes=[
                pltpu.VMEM((rows, dim), BF16),
                pltpu.VMEM((2, rows, 1), F32),
                pltpu.VMEM((nk, seq, KC), BF16),
                pltpu.VMEM((seq, heads * hd3), F32),
                pltpu.VMEM((seq, ff), F32),
                pltpu.VMEM((U_SLOTS, heads, KC, hd3), BF16),
                pltpu.VMEM((U_SLOTS, KC, ff), BF16),
                pltpu.VMEM((D_SLOTS, att + ff, NC), BF16),
                pltpu.VMEM((seq, att + ff), BF16),
                pltpu.VMEM((nj, rows, NC), F32),
                pltpu.VMEM((nj, rows, NC), F32),
                pltpu.VMEM((nj, rows, NC), F32),
                pltpu.VMEM((nj, rows, NC), F32),
                pltpu.VMEM((nj, rows, NC), F32),
                pltpu.VMEM((nj, rows, NC), F32),
                pltpu.VMEM((nj, rows, NC), F32),
                dma, dma((U_SLOTS,)), dma((U_SLOTS,)), dma((D_SLOTS,)), dma((D_SLOTS,)),
                dma((nk,)), dma((nk,)), dma((nk,)), dma((nk,)), dma((nk,)), dma((nk,)),
                dma((nj,)), dma((nj,)), dma((nj,)), dma((nj,)), dma((nj,)), dma((nj,)),
            ],
            compiler_params=pltpu.CompilerParams(
                collective_id=0, has_side_effects=True, vmem_limit_bytes=66_000_000),
            cost_estimate=pl.CostEstimate(flops=32 * 10**9, bytes_accessed=125 * 10**6, transcendentals=10**6),
            name="block",
        )(x_loc, ln_gamma.reshape(1, dim), jnp.transpose(w_qkv, (1, 0, 2)), w_up,
          w_out.reshape(att, dim), w_down)

    row_spec = P(("data", "tp"), None)
    return jax.shard_map(
        local_block, mesh=mesh,
        in_specs=(row_spec, P(None), P(None, "tp", None), P("tp", None, None), P(None, "tp"), P("tp", None)),
        out_specs=row_spec, check_vma=False)
```

time: 74.2 us -> 70.5 us (0.950)
  Pallas kernels: 72.1 us -> 69.5 us
  local copies, waits for them, and re-layouts: 1.97 us -> 0.84 us
    pallas_call x1, Pallas kernels: 72.1 us -> 69.5 us  [local_block(): pl.pallas_call(kernel, out_shape=pltpu.VMEM((rows, dim), BF16), in_specs=...]
    unnamed x1, local copies, waits for them, and re-layouts: 1.97 us -> 0.84 us
where the time goes in v2:
time: 70.5 us; the launch traced here: 70.3 us
  Pallas kernels  69.5 us (99%)
  local copies, waits for them, and re-layouts  0.84 us (1%)
    pallas_call x1, Pallas kernels, local_block(): pl.pallas_call(kernel, out_shape=pltpu.VMEM((rows, dim), BF16), in_specs=...  69.5 us

profile of v2, /device:TPU:0, one launch (start us, length us, event | category | flops | bytes accessed | tf_op | source)
XLA Modules:
  0.0 70.3 jit_solution(9140830086979299997)
XLA Ops:
  0.0 69.5 %block.1 = bf16[64,5120]{1,0:T(8,128)(2,1)S(1)} custom-call(bf16[64,5120]{1,0:T(8,128)(2,1)} %x_hbm.1, f32[1,5120]{1,0:T(1,128)} %bitcast.5, bf16[10,5120,384]{2,1,0:T(8,128)(2,1)} %bitcast.3, bf16[5120,3456]{1,0:T(8,128)(2,1)} %wup_ref.1, bf16[1280,5120]{1,0:T(8,128)(2,1)} %bitcast.4, bf16[3456,5120]{1,0:T(8,128)(2,1)} %wdown_ref.1), custom_call_target="tpu_custom_call" | custom-call | flops 32000000000 | bytes 125000000 | tf_op jit(solution)/shard_map/block/pallas_call | solution.py:295
  69.5 0.8 %copy.8 = bf16[64,5120]{1,0:T(8,128)(2,1)} copy(bf16[64,5120]{1,0:T(8,128)(2,1)S(1)} %block.1) | data formatting | bytes 1310720

commit v3 on v2

v3 whole, which is shorter than its diff:
```python
import jax
import jax.numpy as jnp
from jax import lax
from jax.experimental import pallas as pl
from jax.experimental.pallas import tpu as pltpu
from jax.sharding import PartitionSpec as P

LN_EPS = 1e-6
MESH = pl.DeviceIdType.MESH
F32 = jnp.float32
BF16 = jnp.bfloat16

KC = 512
NC = 384
SLOTS = 5
SPLIT = 3
LATE = 2


def kernel(x_hbm, g_hbm, wqkv_ref, wup_ref, wout_ref, wdown_ref, y_ref,
           x_ref, g_ref, stat, xn, acc_qkv, acc_up, wq_buf, wu_buf, act,
           snd_sc, rcv_sc, snd_so, rcv_so, snd_x, rcv_x, mine,
           sem_in, sem_g, sem_wq, sem_wu, sem_wo, sem_wd,
           s_sib, r_sib, s_par, r_par, s_fwd, r_fwd,
           s_rc, r_rc, s_ro, r_ro, s_rx, r_rx):
    rows, dim = x_ref.shape
    heads, head_dim = wout_ref.shape[:2]
    ff = wup_ref.shape[1]
    att = heads * head_dim
    nk, nj = dim // KC, pl.cdiv(dim, NC)
    ksub, n_out = KC // head_dim, (att + ff) // head_dim
    d = lax.axis_index("data")
    t = lax.axis_index("tp")
    sib = (d, t + 1 - 2 * (t % 2))
    par = (d, (t + 2) % 4)
    scale = head_dim ** -0.5
    near, far = slice(0, 2 * rows), slice(2 * rows, 4 * rows)

    x_in = pltpu.make_async_copy(x_hbm, x_ref, sem_in)
    x_in.start()
    g_in = pltpu.make_async_copy(g_hbm, g_ref, sem_g)
    g_in.start()

    bar = pltpu.get_barrier_semaphore()
    for peer in (sib, par):
        pl.semaphore_signal(bar, inc=1, device_id=peer, device_id_type=MESH)

    def q_copies(k, slot):
        return [pltpu.make_async_copy(
            wqkv_ref.at[h, pl.ds(k * ksub, ksub)], wq_buf.at[slot, pl.ds(h * ksub, ksub)], sem_wq.at[slot, h])
            for h in range(heads)]

    def u_copy(k, slot):
        return pltpu.make_async_copy(wup_ref.at[pl.ds(k * KC, KC), :], wu_buf.at[slot], sem_wu.at[slot])

    def down_copies(j, slot, n=NC):
        src, dst = pl.ds(j * NC, n), pl.ds(0, n)
        return (
            pltpu.make_async_copy(wout_ref.at[:, :, src], wq_buf.at[slot, pl.ds(0, heads), :, dst], sem_wo.at[slot]),
            pltpu.make_async_copy(
                wdown_ref.at[:, :, src], wq_buf.at[slot, pl.ds(heads, n_out - heads), :, dst], sem_wd.at[slot]),
        )

    def remote(src, dst, ssem, rsem, peer):
        return pltpu.make_async_remote_copy(
            src_ref=src, dst_ref=dst, send_sem=ssem, recv_sem=rsem,
            device_id=peer, device_id_type=MESH)

    def blk(r):
        return pl.ds(r * rows, rows)

    def to_sib(k):
        return remote(xn.at[k, blk(0), :], xn.at[k, blk(1), :], s_sib.at[k], r_sib.at[k], sib)

    def to_par(k):
        return remote(xn.at[k, blk(0), :], xn.at[k, blk(2), :], s_par.at[k], r_par.at[k], par)

    def fwd(k):
        return remote(xn.at[k, blk(2), :], xn.at[k, blk(3), :], s_fwd.at[k], r_fwd.at[k], sib)

    def rs_cross(j, n=NC):
        c = pl.ds(0, n)
        return remote(snd_sc.at[j, :, c], rcv_sc.at[j, :, c], s_rc.at[j], r_rc.at[j], sib)

    def rs_own(j, n=NC):
        c = pl.ds(0, n)
        return remote(snd_so.at[j, :, c], rcv_so.at[j, :, c], s_ro.at[j], r_ro.at[j], sib)

    def rs_x(j, n=NC):
        c = pl.ds(0, n)
        return remote(snd_x.at[j, :, c], rcv_x.at[j, :, c], s_rx.at[j], r_rx.at[j], par)

    def start_up(k, slot):
        for c in q_copies(k, slot) + [u_copy(k, slot)]:
            c.start()

    start_up(0, 0)

    x_in.wait()
    for i in range(rows // 16):
        r = slice(i * 16, (i + 1) * 16)
        v = x_ref[r, :].astype(F32)
        mean = jnp.mean(v, axis=-1, keepdims=True)
        cen = v - mean
        var = jnp.mean(cen * cen, axis=-1, keepdims=True)
        stat[0, r, :] = mean
        stat[1, r, :] = lax.rsqrt(var + LN_EPS)

    start_up(1, 1)

    def normalize(k):
        c = slice(k * KC, (k + 1) * KC)
        cen = x_ref[:, c].astype(F32) - stat[0]
        xn[k, 0:rows, :] = (cen * stat[1] * g_ref[:, c]).astype(BF16)

    def send(k):
        to_par(k).start()
        to_sib(k).start()

    g_in.wait()
    normalize(0)
    pl.semaphore_wait(bar, 2)
    start_up(2, 2)
    for k in range(1, nk):
        normalize(k)
        send(k - 1)
    acc_qkv[near] = jnp.zeros_like(acc_qkv[near])
    send(nk - 1)
    acc_qkv[far] = jnp.zeros_like(acc_qkv[far])
    acc_up[...] = jnp.zeros_like(acc_up)

    pair = 2 * 3 * head_dim

    def q_pass(k, slot, r):
        xk = xn[k, r, :]
        for h in range(0, heads, 2):
            w = jnp.concatenate(
                [wq_buf[slot, i * ksub:(i + 1) * ksub].reshape(KC, 3 * head_dim) for i in (h, h + 1)], axis=1)
            sl = slice(h // 2 * pair, (h // 2 + 1) * pair)
            acc_qkv[r, sl] += jnp.dot(xk, w, preferred_element_type=F32)

    def u_pass(k, slot, r, final=False):
        xk = xn[k, r, :]
        for n in range(0, ff, pair):
            end = min(n + pair, ff)
            total = acc_up[r, n:end] + jnp.dot(xk, wu_buf[slot, :, n:end], preferred_element_type=F32)
            if final:
                act[r, att + n:att + end] = jax.nn.gelu(total, approximate=True).astype(BF16)
            else:
                acc_up[r, n:end] = total

    def start_q(k, slot):
        for c in q_copies(k, slot):
            c.start()

    def wait_q(k, slot):
        for c in q_copies(k, slot):
            c.wait()

    def start_down(j, slot, n=NC):
        for c in down_copies(j, slot, n):
            c.start()

    def forward(k):
        to_par(k).wait_recv()
        fwd(k).start()

    early = nk - LATE - SLOTS

    def refill(f, slot):
        start_q(f + SLOTS, slot)

        @pl.when(f < early)
        def _():
            u_copy(f + SLOTS, slot).start()

        @pl.when(f == SLOTS - 1)
        def _():
            for i in range(early, SLOTS):
                u_copy(i + SLOTS, i).start()

    @pl.loop(0, SPLIT + 1)
    def _(k):
        @pl.when(k < SPLIT)
        def _():
            to_sib(k).wait_recv()
            wait_q(k, k)
            u_copy(k, k).wait()

            @pl.when(k + SPLIT < SLOTS)
            def _():
                start_up(k + SPLIT, k + SPLIT)

            q_pass(k, k, near)
            u_pass(k, k, near)

        forward(k)

        @pl.when(k > 0)
        def _():
            f = k - 1
            fwd(f).wait_recv()
            q_pass(f, f, far)
            u_pass(f, f, far)
            refill(f, f)

    def full_waits(k, slot):
        @pl.when(k + 1 < nk)
        def _():
            forward(k + 1)

        to_sib(k).wait_recv()
        fwd(k).wait_recv()
        wait_q(k, slot)

    @pl.loop(SPLIT, SLOTS)
    def _(k):
        full_waits(k, k)
        u_copy(k, k).wait()
        q_pass(k, k, slice(None))
        u_pass(k, k, slice(None))
        refill(k, k)

    @pl.loop(SLOTS, nk - LATE)
    def _(k):
        slot = k - SLOTS
        full_waits(k, slot)
        u_copy(k, slot).wait()
        q_pass(k, slot, slice(None))
        u_pass(k, slot, far)
        start_down(slot, slot)

    @pl.loop(nk - LATE, nk)
    def _(k):
        slot = k - SLOTS
        full_waits(k, slot)
        q_pass(k, slot, slice(None))
        start_down(slot, slot)

    def attention(qr):
        for h in range(heads):
            o = h * 3 * head_dim
            q = acc_qkv[qr, o:o + head_dim].astype(BF16)
            kk = acc_qkv[:, o + head_dim:o + 2 * head_dim].astype(BF16)
            vv = acc_qkv[:, o + 2 * head_dim:o + 3 * head_dim].astype(BF16)
            s = lax.dot_general(q, kk, (((1,), (1,)), ((), ())), preferred_element_type=F32) * scale
            e = jnp.exp(s - jnp.max(s, axis=-1, keepdims=True))
            l = jnp.sum(e, axis=-1, keepdims=True)
            ov = jnp.dot(e.astype(BF16), vv, preferred_element_type=F32)
            act[qr, h * head_dim:(h + 1) * head_dim] = (ov / l).astype(BF16)

    last, n_last = nj - 1, dim - (nj - 1) * NC

    def product(slot, r, n):
        w = wq_buf[slot, 0:n_out, :, 0:n].reshape(att + ff, n)
        return jnp.dot(act[r], w, preferred_element_type=F32)

    def cross(j, slot, n=NC):
        p = product(slot, far, n)
        snd_x[j, :, 0:n] = p[0:rows]
        snd_sc[j, :, 0:n] = p[rows:2 * rows]
        rs_cross(j, n).start()

    def own(j, slot, n=NC):
        p = product(slot, near, n)
        mine[j, :, 0:n] = p[0:rows]
        snd_so[j, :, 0:n] = p[rows:2 * rows]
        rs_own(j, n).start()

    def combine(j, n=NC):
        rs_cross(j, n).wait_recv()
        snd_x[j, :, 0:n] = snd_x[j, :, 0:n] + rcv_sc[j, :, 0:n]
        rs_x(j, n).start()

    def wait_down(j, slot, n=NC):
        for c in down_copies(j, slot, n):
            c.wait()

    for i in range(early, SLOTS):
        u_copy(i + SLOTS, i).wait()
    for i in range(early, SLOTS):
        u_pass(i + SLOTS, i, far, i == SLOTS - 1)
    attention(far)

    @pl.loop(0, 3)
    def _(j):
        wait_down(j, j)
        cross(j, j)

        @pl.loop(jnp.maximum(2 * j - 1, 0), jnp.minimum(2 * j + 1, SLOTS - 1))
        def _(i):
            u_pass(i + SLOTS, i, near)

        combine(j)

    wait_down(3, 3)
    cross(3, 3)
    u_pass(nk - 1, SLOTS - 1, near, True)
    attention(near)
    combine(3)

    def refill_down(j):
        slot = j % SLOTS

        @pl.when(j + SLOTS < last)
        def _():
            start_down(j + SLOTS, slot)

        @pl.when(j + SLOTS == last)
        def _():
            start_down(last, slot, n_last)

    own(0, 0)
    refill_down(0)

    @pl.loop(4, last)
    def _(j):
        wait_down(j, j % SLOTS)
        cross(j, j % SLOTS)
        o = jnp.where(j == 4, 1, j - 2)
        own(o, o % SLOTS)
        combine(j)
        refill_down(o)

        @pl.when(j == 4)
        def _():
            own(2, 2)
            refill_down(2)

    wait_down(last, last % SLOTS, n_last)
    cross(last, last % SLOTS, n_last)
    own(last - 2, (last - 2) % SLOTS)
    combine(last, n_last)
    own(last - 1, (last - 1) % SLOTS)
    own(last, last % SLOTS, n_last)

    for j in range(nj):
        n = n_last if j == last else NC
        cols = slice(j * NC, j * NC + n)
        rs_own(j, n).wait_recv()
        part = x_ref[:, cols].astype(F32) + (mine[j, :, 0:n] + rcv_so[j, :, 0:n])
        rs_x(j, n).wait_recv()
        y_ref[:, cols] = (part + rcv_x[j, :, 0:n]).astype(BF16)

    @pl.loop(0, nk)
    def _(k):
        to_sib(k).wait_send()
        to_par(k).wait_send()
        fwd(k).wait_send()

    for j in range(nj):
        n = n_last if j == last else NC
        rs_cross(j, n).wait_send()
        rs_own(j, n).wait_send()
        rs_x(j, n).wait_send()


def solution(mesh):
    def local_block(x_loc, ln_gamma, w_qkv, w_out, w_up, w_down):
        rows, dim = x_loc.shape
        heads, hd3 = w_qkv.shape[1:]
        hd = hd3 // 3
        att = heads * hd
        ff = w_up.shape[1]
        seq = 4 * rows
        nk, nj = dim // KC, pl.cdiv(dim, NC)
        vm = pl.BlockSpec(memory_space=pltpu.VMEM)
        hbm = pl.BlockSpec(memory_space=pl.ANY)
        dma = pltpu.SemaphoreType.DMA
        return pl.pallas_call(
            kernel,
            out_shape=pltpu.VMEM((rows, dim), BF16),
            in_specs=[hbm, hbm, hbm, hbm, hbm, hbm],
            out_specs=vm,
            scratch_shapes=[
                pltpu.VMEM((rows, dim), BF16),
                pltpu.VMEM((1, dim), F32),
                pltpu.VMEM((2, rows, 1), F32),
                pltpu.VMEM((nk, seq, KC), BF16),
                pltpu.VMEM((seq, heads * hd3), F32),
                pltpu.VMEM((seq, ff), F32),
                pltpu.VMEM((SLOTS, heads * KC // hd, hd, hd3), BF16),
                pltpu.VMEM((SLOTS, KC, ff), BF16),
                pltpu.VMEM((seq, att + ff), BF16),
                pltpu.VMEM((nj, rows, NC), F32),
                pltpu.VMEM((nj, rows, NC), F32),
                pltpu.VMEM((nj, rows, NC), F32),
                pltpu.VMEM((nj, rows, NC), F32),
                pltpu.VMEM((nj, rows, NC), F32),
                pltpu.VMEM((nj, rows, NC), F32),
                pltpu.VMEM((nj, rows, NC), F32),
                dma, dma, dma((SLOTS, heads)), dma((SLOTS,)), dma((SLOTS,)), dma((SLOTS,)),
                dma((nk,)), dma((nk,)), dma((nk,)), dma((nk,)), dma((nk,)), dma((nk,)),
                dma((nj,)), dma((nj,)), dma((nj,)), dma((nj,)), dma((nj,)), dma((nj,)),
            ],
            compiler_params=pltpu.CompilerParams(
                collective_id=0, has_side_effects=True, vmem_limit_bytes=66_000_000),
            cost_estimate=pl.CostEstimate(flops=32 * 10**9, bytes_accessed=125 * 10**6, transcendentals=10**6),
            name="block",
        )(x_loc, ln_gamma.reshape(1, dim), jnp.transpose(w_qkv, (1, 0, 2)).reshape(heads, dim // hd, hd, hd3), w_up,
          w_out, w_down.reshape(ff // hd, hd, dim))

    row_spec = P(("data", "tp"), None)
    return jax.shard_map(
        local_block, mesh=mesh,
        in_specs=(row_spec, P(None), P(None, "tp", None), P("tp", None, None), P(None, "tp"), P("tp", None)),
        out_specs=row_spec, check_vma=False)
```

time: 70.5 us -> 66.6 us (0.945)
  Pallas kernels: 69.5 us -> 65.7 us
    pallas_call x1, Pallas kernels: 69.5 us -> 65.7 us  [local_block(): pl.pallas_call(kernel, out_shape=pltpu.VMEM((rows, dim), BF16), in_specs=...]
where the time goes in v3:
time: 66.6 us; the launch traced here: 66.5 us
  Pallas kernels  65.7 us (99%)
  local copies, waits for them, and re-layouts  0.84 us (1%)
    pallas_call x1, Pallas kernels, local_block(): pl.pallas_call(kernel, out_shape=pltpu.VMEM((rows, dim), BF16), in_specs=...  65.7 us

profile of v3, /device:TPU:0, one launch (start us, length us, event | category | flops | bytes accessed | tf_op | source)
XLA Modules:
  0.0 66.5 jit_solution(4093194243703609794)
XLA Ops:
  0.0 65.7 %block.1 = bf16[64,5120]{1,0:T(8,128)(2,1)S(1)} custom-call(bf16[64,5120]{1,0:T(8,128)(2,1)} %x_hbm.1, f32[1,5120]{1,0:T(1,128)} %bitcast.7, bf16[10,40,128,384]{3,2,1,0:T(8,128)(2,1)} %bitcast.5, bf16[5120,3456]{1,0:T(8,128)(2,1)} %wup_ref.1, bf16[10,128,5120]{2,1,0:T(8,128)(2,1)} %wout_ref.1, bf16[27,128,5120]{2,1,0:T(8,128)(2,1)} %bitcast.6), custom_call_target="tpu_custom_call" | custom-call | flops 32000000000 | bytes 125000000 | tf_op jit(solution)/shard_map/block/pallas_call | solution.py:370
  65.7 0.8 %copy.8 = bf16[64,5120]{1,0:T(8,128)(2,1)} copy(bf16[64,5120]{1,0:T(8,128)(2,1)S(1)} %block.1) | data formatting | bytes 1310720

commit v4 on v3

--- a/solution.py
+++ b/solution.py
@@ -13,8 +13,6 @@
 KC = 512
 NC = 384
 SLOTS = 5
-SPLIT = 3
-LATE = 2
 
 
 def kernel(x_hbm, g_hbm, wqkv_ref, wup_ref, wout_ref, wdown_ref, y_ref,
@@ -131,19 +129,21 @@
 
     pair = 2 * 3 * head_dim
 
-    def q_pass(k, slot, r):
-        xk = xn[k, r, :]
+    def ksum(terms):
+        return sum(jnp.dot(x, w, preferred_element_type=F32) for x, w in terms)
+
+    def q_pass(ks, r):
         for h in range(0, heads, 2):
-            w = jnp.concatenate(
-                [wq_buf[slot, i * ksub:(i + 1) * ksub].reshape(KC, 3 * head_dim) for i in (h, h + 1)], axis=1)
             sl = slice(h // 2 * pair, (h // 2 + 1) * pair)
-            acc_qkv[r, sl] += jnp.dot(xk, w, preferred_element_type=F32)
-
-    def u_pass(k, slot, r, final=False):
-        xk = xn[k, r, :]
+            acc_qkv[r, sl] += ksum(
+                (xn[k, r, :], jnp.concatenate(
+                    [wq_buf[slot, i * ksub:(i + 1) * ksub].reshape(KC, 3 * head_dim) for i in (h, h + 1)], axis=1))
+                for k, slot in ks)
+
+    def u_pass(ks, r, final=False):
         for n in range(0, ff, pair):
             end = min(n + pair, ff)
-            total = acc_up[r, n:end] + jnp.dot(xk, wu_buf[slot, :, n:end], preferred_element_type=F32)
+            total = acc_up[r, n:end] + ksum((xn[k, r, :], wu_buf[slot, :, n:end]) for k, slot in ks)
             if final:
                 act[r, att + n:att + end] = jax.nn.gelu(total, approximate=True).astype(BF16)
             else:
@@ -165,77 +165,90 @@
         to_par(k).wait_recv()
         fwd(k).start()
 
-    early = nk - LATE - SLOTS
-
-    def refill(f, slot):
-        start_q(f + SLOTS, slot)
-
-        @pl.when(f < early)
-        def _():
-            u_copy(f + SLOTS, slot).start()
-
-        @pl.when(f == SLOTS - 1)
-        def _():
-            for i in range(early, SLOTS):
-                u_copy(i + SLOTS, i).start()
-
-    @pl.loop(0, SPLIT + 1)
-    def _(k):
-        @pl.when(k < SPLIT)
-        def _():
-            to_sib(k).wait_recv()
-            wait_q(k, k)
-            u_copy(k, k).wait()
-
-            @pl.when(k + SPLIT < SLOTS)
-            def _():
-                start_up(k + SPLIT, k + SPLIT)
-
-            q_pass(k, k, near)
-            u_pass(k, k, near)
-
-        forward(k)
-
-        @pl.when(k > 0)
-        def _():
-            f = k - 1
-            fwd(f).wait_recv()
-            q_pass(f, f, far)
-            u_pass(f, f, far)
-            refill(f, f)
-
-    def full_waits(k, slot):
-        @pl.when(k + 1 < nk)
-        def _():
-            forward(k + 1)
-
+    everyone = slice(None)
+
+    def next_q(k):
+        start_q(k + SLOTS, k)
+
+    def next_u(k):
+        u_copy(k + SLOTS, k).start()
+
+    def wait_rows(k):
         to_sib(k).wait_recv()
         fwd(k).wait_recv()
-        wait_q(k, slot)
-
-    @pl.loop(SPLIT, SLOTS)
+
+    @pl.loop(0, 3)
     def _(k):
-        full_waits(k, k)
+        to_sib(k).wait_recv()
+        wait_q(k, k)
         u_copy(k, k).wait()
-        q_pass(k, k, slice(None))
-        u_pass(k, k, slice(None))
-        refill(k, k)
-
-    @pl.loop(SLOTS, nk - LATE)
+
+        @pl.when(k + 3 < SLOTS)
+        def _():
+            start_up(k + 3, k + 3)
+
+        q_pass([(k, k)], near)
+        u_pass([(k, k)], near)
+        forward(k + k // 2)
+
+        @pl.when(k == 1)
+        def _():
+            fwd(0).wait_recv()
+            q_pass([(0, 0)], far)
+            u_pass([(0, 0)], far)
+            next_q(0)
+            next_u(0)
+            forward(2)
+
+    fwd(1).wait_recv()
+    fwd(2).wait_recv()
+    q_pass([(1, 1), (2, 2)], far)
+    u_pass([(1, 1), (2, 2)], far)
+    next_q(1)
+    next_u(1)
+    next_q(2)
+    next_u(2)
+    forward(4)
+
+    @pl.loop(3, SLOTS)
     def _(k):
-        slot = k - SLOTS
-        full_waits(k, slot)
-        u_copy(k, slot).wait()
-        q_pass(k, slot, slice(None))
-        u_pass(k, slot, far)
-        start_down(slot, slot)
-
-    @pl.loop(nk - LATE, nk)
-    def _(k):
-        slot = k - SLOTS
-        full_waits(k, slot)
-        q_pass(k, slot, slice(None))
-        start_down(slot, slot)
+        wait_rows(k)
+        wait_q(k, k)
+        u_copy(k, k).wait()
+        q_pass([(k, k)], everyone)
+        u_pass([(k, k)], everyone)
+        next_q(k)
+
+        @pl.when(k == 4)
+        def _():
+            next_u(3)
+            next_u(4)
+
+        forward(2 * k - 1)
+        forward(2 * k)
+
+    for k in (5, 6):
+        wait_rows(k)
+        wait_q(k, k - SLOTS)
+        u_copy(k, k - SLOTS).wait()
+    q_pass([(5, 0), (6, 1)], everyone)
+    u_pass([(5, 0), (6, 1)], far)
+    start_down(0, 0)
+    start_down(1, 1)
+    forward(9)
+    for k in (7, 8):
+        wait_rows(k)
+        wait_q(k, k - SLOTS)
+    u_copy(7, 2).wait()
+    q_pass([(7, 2), (8, 3)], everyone)
+    u_pass([(7, 2)], far)
+    start_down(2, 2)
+    start_down(3, 3)
+    wait_rows(9)
+    wait_q(9, 4)
+    u_copy(8, 3).wait()
+    u_copy(9, 4).wait()
+    q_pass([(9, 4)], everyone)
 
     def attention(qr):
         for h in range(heads):
@@ -276,28 +289,23 @@
         for c in down_copies(j, slot, n):
             c.wait()
 
-    for i in range(early, SLOTS):
-        u_copy(i + SLOTS, i).wait()
-    for i in range(early, SLOTS):
-        u_pass(i + SLOTS, i, far, i == SLOTS - 1)
+    u_pass([(8, 3), (9, 4)], far, True)
     attention(far)
-
-    @pl.loop(0, 3)
-    def _(j):
-        wait_down(j, j)
-        cross(j, j)
-
-        @pl.loop(jnp.maximum(2 * j - 1, 0), jnp.minimum(2 * j + 1, SLOTS - 1))
-        def _(i):
-            u_pass(i + SLOTS, i, near)
-
-        combine(j)
-
-    wait_down(3, 3)
-    cross(3, 3)
-    u_pass(nk - 1, SLOTS - 1, near, True)
+    start_down(4, 4)
+
+    wait_down(0, 0)
+    cross(0, 0)
+    u_pass([(5, 0), (6, 1)], near)
+    combine(0)
+    wait_down(1, 1)
+    cross(1, 1)
+    u_pass([(7, 2), (8, 3)], near)
+    combine(1)
+    wait_down(2, 2)
+    cross(2, 2)
+    u_pass([(9, 4)], near, True)
     attention(near)
-    combine(3)
+    combine(2)
 
     def refill_down(j):
         slot = j % SLOTS
@@ -310,29 +318,48 @@
         def _():
             start_down(last, slot, n_last)
 
+    wait_down(3, 3)
+    cross(3, 3)
     own(0, 0)
+    combine(3)
     refill_down(0)
 
     @pl.loop(4, last)
     def _(j):
         wait_down(j, j % SLOTS)
         cross(j, j % SLOTS)
-        o = jnp.where(j == 4, 1, j - 2)
-        own(o, o % SLOTS)
+        own(j - 3, (j - 3) % SLOTS)
         combine(j)
-        refill_down(o)
-
-        @pl.when(j == 4)
-        def _():
-            own(2, 2)
-            refill_down(2)
+        refill_down(j - 3)
 
     wait_down(last, last % SLOTS, n_last)
     cross(last, last % SLOTS, n_last)
-    own(last - 2, (last - 2) % SLOTS)
+    own(last - 3, (last - 3) % SLOTS)
     combine(last, n_last)
-    own(last - 1, (last - 1) % SLOTS)
+
+    @pl.loop(last - 2, last)
+    def _(j):
+        own(j, j % SLOTS)
+
     own(last, last % SLOTS, n_last)
+
+    @pl.loop(0, nk)
+    def _(k):
+        to_sib(k).wait_send()
+        to_par(k).wait_send()
+        fwd(k).wait_send()
+
+    @pl.loop(0, last)
+    def _(j):
+        rs_cross(j).wait_send()
+        rs_own(j).wait_send()
+
+    @pl.loop(0, last - 2)
+    def _(j):
+        rs_x(j).wait_send()
+
+    rs_cross(last, n_last).wait_send()
+    rs_own(last, n_last).wait_send()
 
     for j in range(nj):
         n = n_last if j == last else NC
@@ -342,17 +369,9 @@
         rs_x(j, n).wait_recv()
         y_ref[:, cols] = (part + rcv_x[j, :, 0:n]).astype(BF16)
 
-    @pl.loop(0, nk)
-    def _(k):
-        to_sib(k).wait_send()
-        to_par(k).wait_send()
-        fwd(k).wait_send()
-
-    for j in range(nj):
-        n = n_last if j == last else NC
-        rs_cross(j, n).wait_send()
-        rs_own(j, n).wait_send()
-        rs_x(j, n).wait_send()
+    rs_x(last - 2).wait_send()
+    rs_x(last - 1).wait_send()
+    rs_x(last, n_last).wait_send()
 
 
 def solution(mesh):

time: 66.6 us -> 63.7 us (0.956)
  Pallas kernels: 65.7 us -> 62.7 us
    pallas_call x1, Pallas kernels: 65.7 us -> 62.7 us  [local_block(): pl.pallas_call(kernel, out_shape=pltpu.VMEM((rows, dim), BF16), in_specs=...]
where the time goes in v4:
time: 63.7 us; the launch traced here: 63.5 us
  Pallas kernels  62.7 us (98%)
  local copies, waits for them, and re-layouts  0.84 us (1%)
    pallas_call x1, Pallas kernels, local_block(): pl.pallas_call(kernel, out_shape=pltpu.VMEM((rows, dim), BF16), in_specs=...  62.7 us

profile of v4, /device:TPU:0, one launch (start us, length us, event | category | flops | bytes accessed | tf_op | source)
XLA Modules:
  0.0 63.5 jit_solution(12393655363820355234)
XLA Ops:
  0.0 62.7 %block.1 = bf16[64,5120]{1,0:T(8,128)(2,1)S(1)} custom-call(bf16[64,5120]{1,0:T(8,128)(2,1)} %x_hbm.1, f32[1,5120]{1,0:T(1,128)} %bitcast.7, bf16[10,40,128,384]{3,2,1,0:T(8,128)(2,1)} %bitcast.5, bf16[5120,3456]{1,0:T(8,128)(2,1)} %wup_ref.1, bf16[10,128,5120]{2,1,0:T(8,128)(2,1)} %wout_ref.1, bf16[27,128,5120]{2,1,0:T(8,128)(2,1)} %bitcast.6), custom_call_target="tpu_custom_call" | custom-call | flops 32000000000 | bytes 125000000 | tf_op jit(solution)/shard_map/block/pallas_call | solution.py:389
  62.7 0.8 %copy.8 = bf16[64,5120]{1,0:T(8,128)(2,1)} copy(bf16[64,5120]{1,0:T(8,128)(2,1)S(1)} %block.1) | data formatting | bytes 1310720

commit v5 on v4

--- a/solution.py
+++ b/solution.py
@@ -18,7 +18,7 @@
 def kernel(x_hbm, g_hbm, wqkv_ref, wup_ref, wout_ref, wdown_ref, y_ref,
            x_ref, g_ref, stat, xn, acc_qkv, acc_up, wq_buf, wu_buf, act,
            snd_sc, rcv_sc, snd_so, rcv_so, snd_x, rcv_x, mine,
-           sem_in, sem_g, sem_wq, sem_wu, sem_wo, sem_wd,
+           sem_in, sem_g, sem_wq, sem_wu, sem_wd,
            s_sib, r_sib, s_par, r_par, s_fwd, r_fwd,
            s_rc, r_rc, s_ro, r_ro, s_rx, r_rx):
     rows, dim = x_ref.shape
@@ -26,6 +26,7 @@
     ff = wup_ref.shape[1]
     att = heads * head_dim
     nk, nj = dim // KC, pl.cdiv(dim, NC)
+    last, n_last = nj - 1, dim - (nj - 1) * NC
     ksub, n_out = KC // head_dim, (att + ff) // head_dim
     d = lax.axis_index("data")
     t = lax.axis_index("tp")
@@ -45,7 +46,7 @@
 
     def q_copies(k, slot):
         return [pltpu.make_async_copy(
-            wqkv_ref.at[h, pl.ds(k * ksub, ksub)], wq_buf.at[slot, pl.ds(h * ksub, ksub)], sem_wq.at[slot, h])
+            wqkv_ref.at[h, pl.ds(k * ksub, ksub)], wq_buf.at[slot, pl.ds(h * ksub, ksub)], sem_wq.at[slot])
             for h in range(heads)]
 
     def u_copy(k, slot):
@@ -54,7 +55,7 @@
     def down_copies(j, slot, n=NC):
         src, dst = pl.ds(j * NC, n), pl.ds(0, n)
         return (
-            pltpu.make_async_copy(wout_ref.at[:, :, src], wq_buf.at[slot, pl.ds(0, heads), :, dst], sem_wo.at[slot]),
+            pltpu.make_async_copy(wout_ref.at[:, :, src], wq_buf.at[slot, pl.ds(0, heads), :, dst], sem_wd.at[slot]),
             pltpu.make_async_copy(
                 wdown_ref.at[:, :, src], wq_buf.at[slot, pl.ds(heads, n_out - heads), :, dst], sem_wd.at[slot]),
         )
@@ -68,25 +69,25 @@
         return pl.ds(r * rows, rows)
 
     def to_sib(k):
-        return remote(xn.at[k, blk(0), :], xn.at[k, blk(1), :], s_sib.at[k], r_sib.at[k], sib)
+        return remote(xn.at[k, blk(0), :], xn.at[k, blk(1), :], s_sib, r_sib.at[k], sib)
 
     def to_par(k):
-        return remote(xn.at[k, blk(0), :], xn.at[k, blk(2), :], s_par.at[k], r_par.at[k], par)
+        return remote(xn.at[k, blk(0), :], xn.at[k, blk(2), :], s_par, r_par.at[k], par)
 
     def fwd(k):
-        return remote(xn.at[k, blk(2), :], xn.at[k, blk(3), :], s_fwd.at[k], r_fwd.at[k], sib)
+        return remote(xn.at[k, blk(2), :], xn.at[k, blk(3), :], s_fwd, r_fwd.at[k], sib)
 
     def rs_cross(j, n=NC):
         c = pl.ds(0, n)
-        return remote(snd_sc.at[j, :, c], rcv_sc.at[j, :, c], s_rc.at[j], r_rc.at[j], sib)
+        return remote(snd_sc.at[j, :, c], rcv_sc.at[j, :, c], s_rc.at[j // last], r_rc.at[j], sib)
 
     def rs_own(j, n=NC):
         c = pl.ds(0, n)
-        return remote(snd_so.at[j, :, c], rcv_so.at[j, :, c], s_ro.at[j], r_ro.at[j], sib)
+        return remote(snd_so.at[j, :, c], rcv_so.at[j, :, c], s_ro.at[j // last], r_ro.at[j // last], sib)
 
     def rs_x(j, n=NC):
         c = pl.ds(0, n)
-        return remote(snd_x.at[j, :, c], rcv_x.at[j, :, c], s_rx.at[j], r_rx.at[j], par)
+        return remote(snd_x.at[j, :, c], rcv_x.at[j, :, c], s_rx.at[j // last], r_rx.at[j], par)
 
     def start_up(k, slot):
         for c in q_copies(k, slot) + [u_copy(k, slot)]:
@@ -154,8 +155,7 @@
             c.start()
 
     def wait_q(k, slot):
-        for c in q_copies(k, slot):
-            c.wait()
+        pltpu.make_async_copy(wq_buf.at[slot], wq_buf.at[slot], sem_wq.at[slot]).wait()
 
     def start_down(j, slot, n=NC):
         for c in down_copies(j, slot, n):
@@ -262,7 +262,6 @@
             ov = jnp.dot(e.astype(BF16), vv, preferred_element_type=F32)
             act[qr, h * head_dim:(h + 1) * head_dim] = (ov / l).astype(BF16)
 
-    last, n_last = nj - 1, dim - (nj - 1) * NC
 
     def product(slot, r, n):
         w = wq_buf[slot, 0:n_out, :, 0:n].reshape(att + ff, n)
@@ -286,8 +285,8 @@
         rs_x(j, n).start()
 
     def wait_down(j, slot, n=NC):
-        for c in down_copies(j, slot, n):
-            c.wait()
+        part = wq_buf.at[slot, pl.ds(0, n_out), :, pl.ds(0, n)]
+        pltpu.make_async_copy(part, part, sem_wd.at[slot]).wait()
 
     u_pass([(8, 3), (9, 4)], far, True)
     attention(far)
@@ -343,34 +342,29 @@
 
     own(last, last % SLOTS, n_last)
 
-    @pl.loop(0, nk)
-    def _(k):
-        to_sib(k).wait_send()
-        to_par(k).wait_send()
-        fwd(k).wait_send()
-
-    @pl.loop(0, last)
-    def _(j):
-        rs_cross(j).wait_send()
-        rs_own(j).wait_send()
-
-    @pl.loop(0, last - 2)
-    def _(j):
-        rs_x(j).wait_send()
-
+    def all_rows(r):
+        return xn.at[:, blk(r), :]
+
+    remote(all_rows(0), all_rows(1), s_sib, r_sib.at[0], sib).wait_send()
+    remote(all_rows(0), all_rows(2), s_par, r_par.at[0], par).wait_send()
+    remote(all_rows(2), all_rows(3), s_fwd, r_fwd.at[0], sib).wait_send()
+    full = pl.ds(0, last)
+    own_all = remote(snd_so.at[full], rcv_so.at[full], s_ro.at[0], r_ro.at[0], sib)
+    remote(snd_sc.at[full], rcv_sc.at[full], s_rc.at[0], r_rc.at[0], sib).wait_send()
     rs_cross(last, n_last).wait_send()
+    own_all.wait_send()
     rs_own(last, n_last).wait_send()
+    own_all.wait_recv()
+    rs_own(last, n_last).wait_recv()
 
     for j in range(nj):
         n = n_last if j == last else NC
         cols = slice(j * NC, j * NC + n)
-        rs_own(j, n).wait_recv()
         part = x_ref[:, cols].astype(F32) + (mine[j, :, 0:n] + rcv_so[j, :, 0:n])
         rs_x(j, n).wait_recv()
         y_ref[:, cols] = (part + rcv_x[j, :, 0:n]).astype(BF16)
 
-    rs_x(last - 2).wait_send()
-    rs_x(last - 1).wait_send()
+    remote(snd_x.at[full], rcv_x.at[full], s_rx.at[0], r_rx.at[0], par).wait_send()
     rs_x(last, n_last).wait_send()
 
 
@@ -408,9 +402,9 @@
                 pltpu.VMEM((nj, rows, NC), F32),
                 pltpu.VMEM((nj, rows, NC), F32),
                 pltpu.VMEM((nj, rows, NC), F32),
-                dma, dma, dma((SLOTS, heads)), dma((SLOTS,)), dma((SLOTS,)), dma((SLOTS,)),
-                dma((nk,)), dma((nk,)), dma((nk,)), dma((nk,)), dma((nk,)), dma((nk,)),
-                dma((nj,)), dma((nj,)), dma((nj,)), dma((nj,)), dma((nj,)), dma((nj,)),
+                dma, dma, dma((SLOTS,)), dma((SLOTS,)), dma((SLOTS,)),
+                dma, dma((nk,)), dma, dma((nk,)), dma, dma((nk,)),
+                dma((2,)), dma((nj,)), dma((2,)), dma((2,)), dma((2,)), dma((nj,)),
             ],
             compiler_params=pltpu.CompilerParams(
                 collective_id=0, has_side_effects=True, vmem_limit_bytes=66_000_000),

time: 63.7 us -> 62.5 us (0.981)
  Pallas kernels: 62.7 us -> 61.5 us
    pallas_call x1, Pallas kernels: 62.7 us -> 61.5 us  [local_block(): pl.pallas_call(kernel, out_shape=pltpu.VMEM((rows, dim), BF16), in_specs=...]
where the time goes in v5:
time: 62.5 us; the launch traced here: 62.3 us
  Pallas kernels  61.5 us (98%)
  local copies, waits for them, and re-layouts  0.84 us (1%)
    pallas_call x1, Pallas kernels, local_block(): pl.pallas_call(kernel, out_shape=pltpu.VMEM((rows, dim), BF16), in_specs=...  61.5 us

profile of v5, /device:TPU:0, one launch (start us, length us, event | category | flops | bytes accessed | tf_op | source)
XLA Modules:
  0.0 62.3 jit_solution(9407663114999350095)
XLA Ops:
  0.0 61.5 %block.1 = bf16[64,5120]{1,0:T(8,128)(2,1)S(1)} custom-call(bf16[64,5120]{1,0:T(8,128)(2,1)} %x_hbm.1, f32[1,5120]{1,0:T(1,128)} %bitcast.7, bf16[10,40,128,384]{3,2,1,0:T(8,128)(2,1)} %bitcast.5, bf16[5120,3456]{1,0:T(8,128)(2,1)} %wup_ref.1, bf16[10,128,5120]{2,1,0:T(8,128)(2,1)} %wout_ref.1, bf16[27,128,5120]{2,1,0:T(8,128)(2,1)} %bitcast.6), custom_call_target="tpu_custom_call" | custom-call | flops 32000000000 | bytes 125000000 | tf_op jit(solution)/shard_map/block/pallas_call | solution.py:383
  61.5 0.8 %copy.8 = bf16[64,5120]{1,0:T(8,128)(2,1)} copy(bf16[64,5120]{1,0:T(8,128)(2,1)S(1)} %block.1) | data formatting | bytes 1310720

commit v6 on v5

--- a/solution.py
+++ b/solution.py
@@ -69,7 +69,7 @@
         return pl.ds(r * rows, rows)
 
     def to_sib(k):
-        return remote(xn.at[k, blk(0), :], xn.at[k, blk(1), :], s_sib, r_sib.at[k], sib)
+        return remote(xn.at[k, blk(0), :], xn.at[k, blk(1), :], s_sib, r_sib.at[k - (k - 3) * ((k + 7) // 10)], sib)
 
     def to_par(k):
         return remote(xn.at[k, blk(0), :], xn.at[k, blk(2), :], s_par, r_par.at[k], par)
@@ -87,7 +87,7 @@
 
     def rs_x(j, n=NC):
         c = pl.ds(0, n)
-        return remote(snd_x.at[j, :, c], rcv_x.at[j, :, c], s_rx.at[j // last], r_rx.at[j], par)
+        return remote(snd_x.at[j, :, c], rcv_x.at[j, :, c], s_rx.at[j // last], r_rx.at[j // 10 * (j - 9)], par)
 
     def start_up(k, slot):
         for c in q_copies(k, slot) + [u_copy(k, slot)]:
@@ -119,7 +119,6 @@
     g_in.wait()
     normalize(0)
     pl.semaphore_wait(bar, 2)
-    start_up(2, 2)
     for k in range(1, nk):
         normalize(k)
         send(k - 1)
@@ -173,8 +172,10 @@
     def next_u(k):
         u_copy(k + SLOTS, k).start()
 
+    late = pl.ds(3, nk - 3)
+    late_sib = remote(xn.at[late, blk(0), :], xn.at[late, blk(1), :], s_sib, r_sib.at[3], sib)
+
     def wait_rows(k):
-        to_sib(k).wait_recv()
         fwd(k).wait_recv()
 
     @pl.loop(0, 3)
@@ -183,10 +184,7 @@
         wait_q(k, k)
         u_copy(k, k).wait()
 
-        @pl.when(k + 3 < SLOTS)
-        def _():
-            start_up(k + 3, k + 3)
-
+        start_up(k + 2, k + 2)
         q_pass([(k, k)], near)
         u_pass([(k, k)], near)
         forward(k + k // 2)
@@ -206,9 +204,8 @@
     u_pass([(1, 1), (2, 2)], far)
     next_q(1)
     next_u(1)
-    next_q(2)
-    next_u(2)
     forward(4)
+    late_sib.wait_recv()
 
     @pl.loop(3, SLOTS)
     def _(k):
@@ -217,6 +214,12 @@
         u_copy(k, k).wait()
         q_pass([(k, k)], everyone)
         u_pass([(k, k)], everyone)
+
+        @pl.when(k == 3)
+        def _():
+            next_q(2)
+            next_u(2)
+
         next_q(k)
 
         @pl.when(k == 4)
@@ -357,11 +360,14 @@
     own_all.wait_recv()
     rs_own(last, n_last).wait_recv()
 
+    ten = pl.ds(0, 10)
+    remote(snd_x.at[ten], rcv_x.at[ten], s_rx.at[0], r_rx.at[0], par).wait_recv()
     for j in range(nj):
         n = n_last if j == last else NC
         cols = slice(j * NC, j * NC + n)
         part = x_ref[:, cols].astype(F32) + (mine[j, :, 0:n] + rcv_so[j, :, 0:n])
-        rs_x(j, n).wait_recv()
+        if j >= 10:
+            rs_x(j, n).wait_recv()
         y_ref[:, cols] = (part + rcv_x[j, :, 0:n]).astype(BF16)
 
     remote(snd_x.at[full], rcv_x.at[full], s_rx.at[0], r_rx.at[0], par).wait_send()
@@ -403,8 +409,8 @@
                 pltpu.VMEM((nj, rows, NC), F32),
                 pltpu.VMEM((nj, rows, NC), F32),
                 dma, dma, dma((SLOTS,)), dma((SLOTS,)), dma((SLOTS,)),
-                dma, dma((nk,)), dma, dma((nk,)), dma, dma((nk,)),
-                dma((2,)), dma((nj,)), dma((2,)), dma((2,)), dma((2,)), dma((nj,)),
+                dma, dma((4,)), dma, dma((nk,)), dma, dma((nk,)),
+                dma((2,)), dma((nj,)), dma((2,)), dma((2,)), dma((2,)), dma((nj - 9,)),
             ],
             compiler_params=pltpu.CompilerParams(
                 collective_id=0, has_side_effects=True, vmem_limit_bytes=66_000_000),

time: 62.5 us -> 61.8 us (0.989)
  Pallas kernels: 61.5 us -> 60.8 us
    pallas_call x1, Pallas kernels: 61.5 us -> 60.8 us  [local_block(): pl.pallas_call(kernel, out_shape=pltpu.VMEM((rows, dim), BF16), in_specs=...]
where the time goes in v6:
time: 61.8 us; the launch traced here: 61.6 us
  Pallas kernels  60.8 us (98%)
  local copies, waits for them, and re-layouts  0.84 us (1%)
    pallas_call x1, Pallas kernels, local_block(): pl.pallas_call(kernel, out_shape=pltpu.VMEM((rows, dim), BF16), in_specs=...  60.8 us

profile of v6, /device:TPU:0, one launch (start us, length us, event | category | flops | bytes accessed | tf_op | source)
XLA Modules:
  0.0 61.6 jit_solution(8493831577789069984)
XLA Ops:
  0.0 60.8 %block.1 = bf16[64,5120]{1,0:T(8,128)(2,1)S(1)} custom-call(bf16[64,5120]{1,0:T(8,128)(2,1)} %x_hbm.1, f32[1,5120]{1,0:T(1,128)} %bitcast.7, bf16[10,40,128,384]{3,2,1,0:T(8,128)(2,1)} %bitcast.5, bf16[5120,3456]{1,0:T(8,128)(2,1)} %wup_ref.1, bf16[10,128,5120]{2,1,0:T(8,128)(2,1)} %wout_ref.1, bf16[27,128,5120]{2,1,0:T(8,128)(2,1)} %bitcast.6), custom_call_target="tpu_custom_call" | custom-call | flops 32000000000 | bytes 125000000 | tf_op jit(solution)/shard_map/block/pallas_call | solution.py:389
  60.8 0.8 %copy.8 = bf16[64,5120]{1,0:T(8,128)(2,1)} copy(bf16[64,5120]{1,0:T(8,128)(2,1)S(1)} %block.1) | data formatting | bytes 1310720

commit v7 on v6

--- a/solution.py
+++ b/solution.py
@@ -18,7 +18,7 @@
 def kernel(x_hbm, g_hbm, wqkv_ref, wup_ref, wout_ref, wdown_ref, y_ref,
            x_ref, g_ref, stat, xn, acc_qkv, acc_up, wq_buf, wu_buf, act,
            snd_sc, rcv_sc, snd_so, rcv_so, snd_x, rcv_x, mine,
-           sem_in, sem_g, sem_wq, sem_wu, sem_wd,
+           sem_in, sem_g, sem_wq, sem_wu,
            s_sib, r_sib, s_par, r_par, s_fwd, r_fwd,
            s_rc, r_rc, s_ro, r_ro, s_rx, r_rx):
     rows, dim = x_ref.shape
@@ -55,9 +55,9 @@
     def down_copies(j, slot, n=NC):
         src, dst = pl.ds(j * NC, n), pl.ds(0, n)
         return (
-            pltpu.make_async_copy(wout_ref.at[:, :, src], wq_buf.at[slot, pl.ds(0, heads), :, dst], sem_wd.at[slot]),
+            pltpu.make_async_copy(wout_ref.at[:, :, src], wq_buf.at[slot, pl.ds(0, heads), :, dst], sem_wq.at[slot]),
             pltpu.make_async_copy(
-                wdown_ref.at[:, :, src], wq_buf.at[slot, pl.ds(heads, n_out - heads), :, dst], sem_wd.at[slot]),
+                wdown_ref.at[:, :, src], wq_buf.at[slot, pl.ds(heads, n_out - heads), :, dst], sem_wq.at[slot]),
         )
 
     def remote(src, dst, ssem, rsem, peer):
@@ -289,7 +289,7 @@
 
     def wait_down(j, slot, n=NC):
         part = wq_buf.at[slot, pl.ds(0, n_out), :, pl.ds(0, n)]
-        pltpu.make_async_copy(part, part, sem_wd.at[slot]).wait()
+        pltpu.make_async_copy(part, part, sem_wq.at[slot]).wait()
 
     u_pass([(8, 3), (9, 4)], far, True)
     attention(far)
@@ -408,7 +408,7 @@
                 pltpu.VMEM((nj, rows, NC), F32),
                 pltpu.VMEM((nj, rows, NC), F32),
                 pltpu.VMEM((nj, rows, NC), F32),
-                dma, dma, dma((SLOTS,)), dma((SLOTS,)), dma((SLOTS,)),
+                dma, dma, dma((SLOTS,)), dma((SLOTS,)),
                 dma, dma((4,)), dma, dma((nk,)), dma, dma((nk,)),
                 dma((2,)), dma((nj,)), dma((2,)), dma((2,)), dma((2,)), dma((nj - 9,)),
             ],

time: 61.8 us -> 61.7 us (level)
  no operation moved by 1% of the time
where the time goes in v7:
time: 61.7 us; the launch traced here: 61.6 us
  Pallas kernels  60.7 us (98%)
  local copies, waits for them, and re-layouts  0.84 us (1%)
    pallas_call x1, Pallas kernels, local_block(): pl.pallas_call(kernel, out_shape=pltpu.VMEM((rows, dim), BF16), in_specs=...  60.7 us

profile of v7, /device:TPU:0, one launch (start us, length us, event | category | flops | bytes accessed | tf_op | source)
XLA Modules:
  0.0 61.6 jit_solution(6746401925552335027)
XLA Ops:
  0.0 60.7 %block.1 = bf16[64,5120]{1,0:T(8,128)(2,1)S(1)} custom-call(bf16[64,5120]{1,0:T(8,128)(2,1)} %x_hbm.1, f32[1,5120]{1,0:T(1,128)} %bitcast.7, bf16[10,40,128,384]{3,2,1,0:T(8,128)(2,1)} %bitcast.5, bf16[5120,3456]{1,0:T(8,128)(2,1)} %wup_ref.1, bf16[10,128,5120]{2,1,0:T(8,128)(2,1)} %wout_ref.1, bf16[27,128,5120]{2,1,0:T(8,128)(2,1)} %bitcast.6), custom_call_target="tpu_custom_call" | custom-call | flops 32000000000 | bytes 125000000 | tf_op jit(solution)/shard_map/block/pallas_call | solution.py:389
  60.7 0.8 %copy.8 = bf16[64,5120]{1,0:T(8,128)(2,1)} copy(bf16[64,5120]{1,0:T(8,128)(2,1)S(1)} %block.1) | data formatting | bytes 1310720
